TPU v7x, 32 devices: a whole 2x2x4 slice. The times are simulated.
32 devices in a mesh: segment: 8 (over z, x), dp: 4 (over y, core).
Axes of the slice: x: 2, y: 2, z: 4, core: 2. Of those that a mesh axis runs over, the one named last changes fastest.
Arguments:
- src_embed: bfloat16 [16, 128, 2048], P('dp', None, 'segment'), parts along dimension 0, may hold values from -6 to 6
- tgt_embed: bfloat16 [16, 128, 2048], P('dp', None, 'segment'), parts along dimension 0, may hold values from -6 to 6
- src_lengths: int32 [16], P('dp'), parts along dimension 0, may hold values from 32 to 128
- tgt_lengths: int32 [16], P('dp'), parts along dimension 0, may hold values from 32 to 128
- attn_in: bfloat16 [8, 2048, 3072], P('segment'), may hold values from -0.125 to 0.125
- attn_out: bfloat16 [8, 1024, 2048], P('segment'), may hold values from -0.375 to 0.375
- norm_gain: float32 [4, 2048], replicated, may hold values from 0.25 to 1.75
- final_gain: float32 [2048], replicated, may hold values from 0.25 to 1.75
Outputs:
- decoded: bfloat16 [16, 128, 2048], P('dp', None, 'segment'), parts along dimension 0
There are 4 independent parts, one for each index of `dp`. A program takes and returns all parts, laid end to end along the dimension named above; an argument that names none is the same for every part. Nothing has to cross between parts.
Inputs may be any that keep to these rules, and one draw needn't show every extreme that they name: `src_lengths`: keys at positions below a sequence's length are its real tokens. `tgt_lengths`: keys at positions below a sequence's length are its real tokens.
All inputs are finite; a program needn't handle non-finite values.
Results may differ from a plain program's by a relative error of at most 0.015.
Values may be sent and summed in bfloat16 or wider, within the bound.
A program may use at most 64 MiB of HBM per device.

v0:
```python
import functools

import jax
import jax.numpy as jnp
from jax import lax
from jax.experimental import pallas as pl
from jax.experimental.pallas import tpu as pltpu
from jax.sharding import PartitionSpec as P

HEAD = 64
LAYERS = 4
MESH = pl.DeviceIdType.MESH
epsilon = 1e-06
score_scale = 0.125


def kernel(
    segs,
    src_len,
    tgt_len,
    src,
    tgt,
    w_in,
    w_out,
    gains,
    final_gain,
    out,
    win,
    wout,
    act,
    nrm,
    qkv,
    mix,
    own,
    ps,
    pr,
    fw,
    w_sem,
    act_sem,
    in_send,
    p_send,
    p_recv,
    f_send,
    o_recv,
    go,
    side,
    side_send,
    side_recv,
    on_send,
    r_send,
):
    group = segs // LAYERS
    batches, seq, cw = src.shape
    width = segs * cw
    hc = wout.shape[0]
    me = lax.axis_index("segment")
    section = me // group
    member = me % group
    is_cross = section == 2
    is_last = section == LAYERS - 1
    q_src = jnp.where(is_cross, 1, 0)

    win_copy = pltpu.make_async_copy(w_in, win, w_sem.at[0])
    wout_copy = pltpu.make_async_copy(w_out, wout, w_sem.at[1])
    win_copy.start()
    wout_copy.start()

    barrier = pltpu.get_barrier_semaphore()
    for step in range(1, segs):
        pl.semaphore_signal(
            barrier,
            inc=1,
            device_id={"segment": lax.rem(me + step, segs)},
            device_id_type=MESH,
        )
    pl.semaphore_wait(barrier, segs - 1)

    def remote(source, dest, send, recv, target):
        return pltpu.make_async_remote_copy(
            src_ref=source,
            dst_ref=dest,
            send_sem=send,
            recv_sem=recv,
            device_id={"segment": target},
            device_id_type=MESH,
        )

    def input_copy(kind, m, j):
        ref = src if kind == 0 else tgt
        target = 2 * kind * group + j
        return remote(
            ref.at[m],
            act.at[kind, m, me],
            in_send.at[kind, m, j],
            act_sem.at[kind, m, me],
            target,
        )

    def sends(kind, m, j):
        if kind == 1:
            return jnp.bool_(True)
        return jnp.logical_or(j == member, jnp.logical_and(section == 0, m > 0))

    def send_inputs(kind, m):
        ref = src if kind == 0 else tgt
        for j in range(group):
            target = 2 * kind * group + j

            @pl.when(jnp.logical_and(sends(kind, m, j), me != target))
            def _():
                input_copy(kind, m, j).start()

            @pl.when(me == target)
            def _():
                pltpu.make_async_copy(
                    ref.at[m], act.at[kind, m, me], act_sem.at[kind, m, me]
                ).start()

    def beside(g):
        return section * group + lax.rem(member + g, group)

    def side_copy(m, g):
        return remote(
            src.at[m],
            side.at[m - 1, g - 1],
            side_send.at[m - 1, g - 1],
            side_recv.at[m - 1, g - 1],
            beside(g),
        )

    def side_on(m, g):
        source = beside(group - g)
        return remote(
            side.at[m - 1, g - 1],
            act.at[0, m, source],
            on_send.at[m - 1, g - 1],
            act_sem.at[0, m, source],
            member,
        )

    def relay(c, g):
        return remote(
            act.at[0, 0, c],
            act.at[0, 0, c],
            r_send.at[g - 1, c],
            act_sem.at[0, 0, c],
            beside(g),
        )

    send_inputs(0, 0)

    @pl.when(section > 0)
    def _():
        for m in range(1, batches):
            for g in range(1, group):
                side_copy(m, g).start()

    @pl.when(section <= 2)
    def _():
        for m in range(batches):
            send_inputs(1, m)

    def act_wait(kind, m, c):
        pltpu.make_async_copy(
            act.at[kind, m, c], act.at[kind, m, c], act_sem.at[kind, m, c]
        ).wait()

    def pass_on():
        for c in range(segs):

            @pl.when(c % group == member)
            def _(c=c):
                act_wait(0, 0, c)
                for g in range(1, group):
                    relay(c, g).start()

    @pl.when(section == 0)
    def _():
        pass_on()
        for step in range(1, segs):
            pl.semaphore_signal(
                go,
                inc=1,
                device_id={"segment": lax.rem(me + step, segs)},
                device_id_type=MESH,
            )

    pl.semaphore_wait(go, jnp.where(section == 0, group - 1, group))
    for m in range(1, batches):
        send_inputs(0, m)

        @pl.when(section > 0)
        def _(m=m):
            for g in range(1, group):
                side_copy(m, g).wait_recv()
                side_on(m, g).start()

    @pl.when(section > 2)
    def _():
        for m in range(batches):
            send_inputs(1, m)

    def normalize(kind, m, gain_row):
        total = jnp.zeros((seq, cw), jnp.float32)
        for c in range(segs):
            v = act[kind, m, c].astype(jnp.float32)
            total = total + v * v
        mean = jnp.sum(total, axis=-1, keepdims=True) * (1.0 / width)
        scale = lax.rsqrt(mean + epsilon)
        for c in range(segs):
            v = act[kind, m, c].astype(jnp.float32)
            g = gain_row(c)
            nrm[kind, :, c * cw : (c + 1) * cw] = (v * scale * g).astype(jnp.bfloat16)

    def key_gain(c):
        cols = slice(c * cw, (c + 1) * cw)
        picked = jnp.where(is_cross, final_gain[:, cols], gains[0:1, cols])
        for p in (1, 3):
            picked = jnp.where(section == p, gains[p : p + 1, cols], picked)
        return picked

    def query_gain(c):
        return gains[2:3, c * cw : (c + 1) * cw]

    def part_copy(m, c, g):
        target = section * group + lax.rem(member + g, group)
        return remote(
            ps.at[m, c],
            pr.at[m, g - 1, c],
            p_send.at[m, g - 1, c],
            p_recv.at[m, g - 1, c],
            target,
        )

    def whole(m):
        return jnp.logical_and(section < LAYERS - 1, m > 0)

    def part_needed(m, c, g):
        goal = lax.rem(member + g, group)
        return jnp.logical_or(whole(m), lax.rem(c, group) == goal)

    def keeps(m, c):
        return jnp.logical_or(whole(m), lax.rem(c, group) == member)

    def next_copy(m, c):
        return remote(
            fw.at[m, c], act.at[0, m, c], f_send.at[m, c], act_sem.at[0, m, c], me + group
        )

    def out_copy(m, c):
        return remote(fw.at[m, c], out.at[m], f_send.at[m, c], o_recv.at[m], c)

    tile = min(512, hc)
    kv_tiles = 2 * hc // tile
    q_tiles = hc // tile

    def prepare(m):
        @pl.when(is_cross)
        def _():
            for c in range(segs):
                act_wait(1, m, c)
            normalize(1, m, query_gain)

        @pl.when(jnp.logical_and(section > 0, m == 0))
        def _():
            pass_on()

        for c in range(segs):

            @pl.when(jnp.logical_or(m > 0, c % group != member))
            def _(c=c):
                act_wait(0, m, c)

        normalize(0, m, key_gain)

        @pl.when(m == 0)
        def _():
            win_copy.wait()


    def project(t, carry):
        kind = jnp.where(t < q_tiles, q_src, 0)
        cols = pl.ds(pl.multiple_of(t * tile, tile), tile)
        qkv[:, cols] = jnp.dot(
            nrm[kind], win[:, cols], preferred_element_type=jnp.float32
        ).astype(jnp.bfloat16)
        return carry

    def attend(m):
        length = jnp.where(is_last, tgt_len[m], src_len[m])
        keys = lax.broadcasted_iota(jnp.int32, (2 * seq, seq), 1)
        rows = lax.broadcasted_iota(jnp.int32, (2 * seq, seq), 0)
        rows = jnp.where(rows >= seq, rows - seq, rows)
        bound = jnp.where(is_last, rows, seq)
        allowed = (keys < length) & (keys <= bound)
        lane = lax.broadcasted_iota(jnp.int32, (seq, 2 * HEAD), 1)
        low = lane < HEAD
        for h in range(hc // (2 * HEAD)):
            at = h * 2 * HEAD
            q2 = qkv[:, at : at + 2 * HEAD]
            k2 = qkv[:, hc + at : hc + at + 2 * HEAD]
            v2 = qkv[:, 2 * hc + at : 2 * hc + at + 2 * HEAD]
            zero = jnp.zeros_like(q2)
            both = jnp.concatenate(
                [jnp.where(low, q2, zero), jnp.where(low, zero, q2)], axis=0
            )
            scores = (
                lax.dot_general(
                    both,
                    k2,
                    (((1,), (1,)), ((), ())),
                    preferred_element_type=jnp.float32,
                )
                * score_scale
            )
            scores = jnp.where(allowed, scores, -1000000000.0)
            top = jnp.max(scores, axis=-1, keepdims=True)
            e = jnp.exp(scores - top)
            weights = (e / jnp.sum(e, axis=-1, keepdims=True)).astype(jnp.bfloat16)
            o = jnp.dot(weights, v2, preferred_element_type=jnp.float32)
            mix[:, at : at + 2 * HEAD] = jnp.where(low, o[:seq], o[seq:]).astype(
                jnp.bfloat16
            )

    def send_parts(m):
        @pl.when(m == 0)
        def _():
            wout_copy.wait()

        def emit(c, carry):
            cols = pl.ds(pl.multiple_of(c * cw, cw), cw)
            part = jnp.dot(mix[...], wout[:, cols], preferred_element_type=jnp.float32)
            own[c] = part
            ps[m, c] = part.astype(jnp.bfloat16)
            for g in range(1, group):

                @pl.when(part_needed(m, c, g))
                def _():
                    part_copy(m, c, g).start()

            return carry

        lax.fori_loop(0, segs, emit, 0, unroll=True)

    def combine(m, c):
        @pl.when(keeps(m, c))
        def _():
            total = own[c] + act[q_src, m, c].astype(jnp.float32)
            for g in range(1, group):
                part_copy(m, c, g).wait_recv()
                total = total + pr[m, g - 1, c].astype(jnp.float32)
            fw[m, c] = total.astype(jnp.bfloat16)

            @pl.when(section < LAYERS - 1)
            def _():
                next_copy(m, c).start()

            @pl.when(jnp.logical_and(is_last, me != c))
            def _():
                out_copy(m, c).start()

            @pl.when(jnp.logical_and(is_last, me == c))
            def _():
                pltpu.make_async_copy(fw.at[m, c], out.at[m], o_recv.at[m]).start()

    half = (q_tiles + kv_tiles) // 2
    stages = (
        prepare,
        lambda m: lax.fori_loop(0, half, project, 0, unroll=True),
        lambda m: lax.fori_loop(half, q_tiles + kv_tiles, project, 0, unroll=True),
        attend,
    )

    def batch_step(t, carry):
        m = t - 1

        @pl.when(t > 0)
        def _():
            send_parts(m)

        for c in range(segs):
            for i, stage in enumerate(stages):
                if c == segs // 2 + i * segs // 8:

                    @pl.when(t < batches)
                    def _(stage=stage):
                        stage(t)

            @pl.when(t > 0)
            def _(c=c):
                combine(m, c)

        return carry

    lax.fori_loop(0, batches + 1, batch_step, 0)

    def finish(m, carry):
        for kind in range(2):
            for j in range(group):

                @pl.when(jnp.logical_and(sends(kind, m, j), me != 2 * kind * group + j))
                def _():
                    input_copy(kind, m, j).wait_send()

        @pl.when(jnp.logical_and(section > 0, m > 0))
        def _():
            for g in range(1, group):
                side_copy(m, g).wait_send()
                side_on(m, g).wait_send()

        def drain(c, carry):
            for g in range(1, group):

                @pl.when(part_needed(m, c, g))
                def _():
                    part_copy(m, c, g).wait_send()

            @pl.when(jnp.logical_and(section < LAYERS - 1, keeps(m, c)))
            def _():
                next_copy(m, c).wait_send()

            @pl.when(jnp.logical_and(m == 0, lax.rem(c, group) == member))
            def _():
                for g in range(1, group):
                    relay(c, g).wait_send()

            @pl.when(jnp.logical_and(is_last, jnp.logical_and(keeps(m, c), me != c)))
            def _():
                out_copy(m, c).wait_send()

            return carry

        lax.fori_loop(0, segs, drain, 0)
        pltpu.make_async_copy(out.at[m], out.at[m], o_recv.at[m]).wait()
        return carry

    lax.fori_loop(0, batches, finish, 0)


def solution(mesh):
    segs = mesh.shape["segment"]

    def on_device(src, tgt, src_len, tgt_len, w_in, w_out, gains, final_gain):
        batches, seq, cw = src.shape
        group = segs // LAYERS
        w_in, w_out = w_in[0], w_out[0]
        width, qkv_cols = w_in.shape
        hc = w_out.shape[0]
        vmem = pl.BlockSpec(memory_space=pltpu.VMEM)
        smem = pl.BlockSpec(memory_space=pltpu.SMEM)
        anym = pl.BlockSpec(memory_space=pl.ANY)
        bf16 = jnp.bfloat16
        block = (segs, seq, cw)
        dma = pltpu.SemaphoreType.DMA
        return pl.pallas_call(
            functools.partial(kernel, segs),
            out_shape=jax.ShapeDtypeStruct(src.shape, src.dtype),
            in_specs=[smem, smem, vmem, vmem, anym, anym, vmem, vmem],
            out_specs=vmem,
            scratch_shapes=[
                pltpu.VMEM((width, qkv_cols), bf16),
                pltpu.VMEM((hc, width), bf16),
                pltpu.VMEM((2, batches) + block, bf16),
                pltpu.VMEM((2, seq, width), bf16),
                pltpu.VMEM((seq, qkv_cols), bf16),
                pltpu.VMEM((seq, hc), bf16),
                pltpu.VMEM(block, jnp.float32),
                pltpu.VMEM((batches,) + block, bf16),
                pltpu.VMEM((batches, group - 1) + block, bf16),
                pltpu.VMEM((batches,) + block, bf16),
                dma((2,)),
                dma((2, batches, segs)),
                dma((2, batches, group)),
                dma((batches, group - 1, segs)),
                dma((batches, group - 1, segs)),
                dma((batches, segs)),
                dma((batches,)),
                pltpu.SemaphoreType.REGULAR,
                pltpu.VMEM((batches - 1, group - 1, seq, cw), bf16),
                dma((batches - 1, group - 1)),
                dma((batches - 1, group - 1)),
                dma((batches - 1, group - 1)),
                dma((group - 1, segs)),
            ],
            compiler_params=pltpu.CompilerParams(
                collective_id=0,
                has_side_effects=True,
                vmem_limit_bytes=56 * 1024 * 1024,
            ),
        )(src_len, tgt_len, src, tgt, w_in, w_out, gains, final_gain[None])

    return jax.shard_map(
        on_device,
        mesh=mesh,
        in_specs=(
            P("dp", None, "segment"),
            P("dp", None, "segment"),
            P("dp"),
            P("dp"),
            P("segment", None, None),
            P("segment", None, None),
            P(),
            P(),
        ),
        out_specs=P("dp", None, "segment"),
        check_vma=False,
    )
```

profile of v0, /device:TPU:0, one launch (start us, length us, event | category | flops | bytes accessed | tf_op | source)
XLA Modules:
  0.0 131.0 jit_solution(11911070578014598525)
XLA Ops:
  0.0 129.4 %shard_map.82 = bf16[4,128,256]{2,1,0:T(8,128)(2,1)} custom-call(s32[4]{0:T(128)} %src_len.1, s32[4]{0:T(128)} %tgt_len.1, bf16[4,128,256]{2,1,0:T(8,128)(2,1)} %src.1, bf16[4,128,256]{2,1,0:T(8,128)(2,1)} %tgt.1, bf16[2048,3072]{1,0:T(8,128)(2,1)} %bitcast.3, bf16[1024,2048]{1,0:T(8,128)(2,1)} %bitcast.4, f32[4,2048]{1,0:T(4,128)} %gains.1, f32[1,2048]{1,0:T(1,128)} %bitcast.5), custom_call_target="tpu_custom_call" | custom-call | tf_op jit(solution)/shard_map/pallas_call | solution.py:455
  129.4 1.7 %copy.10 = bf16[4,128,256]{2,1,0:T(8,128)(2,1)} copy(bf16[4,128,256]{2,1,0:T(8,128)(2,1)} %shard_map.82) | data formatting | bytes 524288
where the time goes:
time: 131 us
  Pallas kernels  129 us (98%)
  local copies, waits for them, and re-layouts  1.67 us (1%)
    pallas_call x1, Pallas kernels, on_device(): pl.pallas_call(functools.partial(kernel, segs), out_shape=jax.ShapeDtypeS...  129 us

commit v1 on v0

--- a/solution.py
+++ b/solution.py
@@ -10,6 +10,18 @@
 HEAD = 64
 LAYERS = 4
 MESH = pl.DeviceIdType.MESH
+SENT = 2
+PLAN = (
+    ("turn", 0),
+    ("combine", 0),
+    ("combine", 1),
+    ("combine", 2),
+    ("combine", 3),
+    ("stage", 0),
+    ("stage", 1),
+    ("stage", 2),
+    ("stage", 3),
+)
 epsilon = 1e-06
 score_scale = 0.125
 
@@ -48,6 +60,8 @@
     side_recv,
     on_send,
     r_send,
+    t_send,
+    turn,
 ):
     group = segs // LAYERS
     batches, seq, cw = src.shape
@@ -73,7 +87,13 @@
             device_id={"segment": lax.rem(me + step, segs)},
             device_id_type=MESH,
         )
-    pl.semaphore_wait(barrier, segs - 1)
+    lane_at = lax.axis_index("dp")
+    leads = lane_at % 2 == 1
+    mate = lane_at + 1 - 2 * (lane_at % 2)
+    pl.semaphore_signal(
+        barrier, inc=1, device_id={"dp": mate}, device_id_type=MESH
+    )
+    pl.semaphore_wait(barrier, segs)
 
     def remote(source, dest, send, recv, target):
         return pltpu.make_async_remote_copy(
@@ -98,7 +118,7 @@
 
     def sends(kind, m, j):
         if kind == 1:
-            return jnp.bool_(True)
+            return jnp.logical_or(j == member, is_cross)
         return jnp.logical_or(j == member, jnp.logical_and(section == 0, m > 0))
 
     def send_inputs(kind, m):
@@ -138,12 +158,12 @@
             member,
         )
 
-    def relay(c, g):
+    def relay(m, c, g):
         return remote(
-            act.at[0, 0, c],
-            act.at[0, 0, c],
-            r_send.at[g - 1, c],
-            act_sem.at[0, 0, c],
+            act.at[0, m, c],
+            act.at[0, m, c],
+            r_send.at[m, g - 1, c],
+            act_sem.at[0, m, c],
             beside(g),
         )
 
@@ -165,28 +185,63 @@
             act.at[kind, m, c], act.at[kind, m, c], act_sem.at[kind, m, c]
         ).wait()
 
-    def pass_on():
-        for c in range(segs):
+    def pass_on(m, order):
+        for c in order:
 
             @pl.when(c % group == member)
             def _(c=c):
-                act_wait(0, 0, c)
+                act_wait(0, m, c)
                 for g in range(1, group):
-                    relay(c, g).start()
+                    relay(m, c, g).start()
+
+    def release(k, first):
+        for c in range(first * group, segs):
+
+            @pl.when(me != c)
+            def _(c=c):
+                pl.semaphore_signal(
+                    go.at[k - 1],
+                    inc=1,
+                    device_id={"segment": c},
+                    device_id_type=MESH,
+                )
 
     @pl.when(section == 0)
     def _():
-        pass_on()
-        for step in range(1, segs):
-            pl.semaphore_signal(
-                go,
-                inc=1,
-                device_id={"segment": lax.rem(me + step, segs)},
-                device_id_type=MESH,
-            )
-
-    pl.semaphore_wait(go, jnp.where(section == 0, group - 1, group))
+        pass_on(0, tuple(range(group)) + tuple(range(segs - 1, 2 * group - 1, -1)))
+        release(1, 0)
+        pass_on(0, range(group, 2 * group))
+
+    def cross_relay(m, c, g):
+        return remote(
+            act.at[1, m, c],
+            act.at[1, m, c],
+            t_send.at[m, g - 1, c],
+            act_sem.at[1, m, c],
+            beside(g),
+        )
+
+    def spread_targets(planes):
+        for m in range(batches):
+            for p in planes:
+                for c in range(p * group, (p + 1) * group):
+
+                    @pl.when(jnp.logical_and(is_cross, c % group == member))
+                    def _(m=m, c=c, p=p):
+                        act_wait(1, m, c)
+                        if p != 2:
+                            for g in range(1, group):
+                                cross_relay(m, c, g).start()
+
+    pl.semaphore_wait(go.at[0], jnp.where(section == 0, group - 1, group))
     for m in range(1, batches):
+        if m > 1:
+            first = 1 if m == 2 else 2
+
+            @pl.when(section >= first)
+            def _(m=m):
+                pl.semaphore_wait(go.at[m - 1], group)
+
         send_inputs(0, m)
 
         @pl.when(section > 0)
@@ -195,10 +250,17 @@
                 side_copy(m, g).wait_recv()
                 side_on(m, g).start()
 
-    @pl.when(section > 2)
-    def _():
-        for m in range(batches):
-            send_inputs(1, m)
+        if m == 1:
+
+            @pl.when(section > 2)
+            def _():
+                for k in range(batches):
+                    send_inputs(1, k)
+
+            spread_targets((2, 1, 0))
+
+        if m == min(2, batches - 1):
+            spread_targets((3,))
 
     def normalize(kind, m, gain_row):
         total = jnp.zeros((seq, cw), jnp.float32)
@@ -232,8 +294,16 @@
             target,
         )
 
+    def whole_from(p, m):
+        inner = m > 0
+        return jnp.logical_and(p < LAYERS - 1, inner)
+
     def whole(m):
-        return jnp.logical_and(section < LAYERS - 1, m > 0)
+        return whole_from(section, m)
+
+    def halved(m):
+        later = jnp.logical_and(section > 0, jnp.logical_not(whole_from(section - 1, m)))
+        return jnp.logical_or(m == 0, later)
 
     def part_needed(m, c, g):
         goal = lax.rem(member + g, group)
@@ -258,16 +328,20 @@
         @pl.when(is_cross)
         def _():
             for c in range(segs):
-                act_wait(1, m, c)
+
+                @pl.when(c % group != member)
+                def _(c=c):
+                    act_wait(1, m, c)
+
             normalize(1, m, query_gain)
 
         @pl.when(jnp.logical_and(section > 0, m == 0))
         def _():
-            pass_on()
+            pass_on(0, range(segs))
 
         for c in range(segs):
 
-            @pl.when(jnp.logical_or(m > 0, c % group != member))
+            @pl.when(jnp.logical_not(jnp.logical_and(halved(m), c % group == member)))
             def _(c=c):
                 act_wait(0, m, c)
 
@@ -332,6 +406,11 @@
             part = jnp.dot(mix[...], wout[:, cols], preferred_element_type=jnp.float32)
             own[c] = part
             ps[m, c] = part.astype(jnp.bfloat16)
+
+            @pl.when(jnp.logical_and(c == 0, jnp.logical_or(m > 0, jnp.logical_not(leads))))
+            def _():
+                pl.semaphore_wait(turn, 1)
+
             for g in range(1, group):
 
                 @pl.when(part_needed(m, c, g))
@@ -341,6 +420,20 @@
             return carry
 
         lax.fori_loop(0, segs, emit, 0, unroll=True)
+
+    def hand_over(m):
+        for c in range(SENT):
+            for g in range(1, group):
+
+                @pl.when(part_needed(m, c, g))
+                def _(c=c, g=g):
+                    part_copy(m, c, g).wait_send()
+
+        @pl.when(jnp.logical_or(m < batches - 1, leads))
+        def _():
+            pl.semaphore_signal(
+                turn, inc=1, device_id={"dp": mate}, device_id_type=MESH
+            )
 
     def combine(m, c):
         @pl.when(keeps(m, c))
@@ -373,22 +466,44 @@
 
     def batch_step(t, carry):
         m = t - 1
+        active = t < batches
 
         @pl.when(t > 0)
         def _():
             send_parts(m)
 
-        for c in range(segs):
-            for i, stage in enumerate(stages):
-                if c == segs // 2 + i * segs // 8:
-
-                    @pl.when(t < batches)
-                    def _(stage=stage):
-                        stage(t)
-
-            @pl.when(t > 0)
-            def _(c=c):
-                combine(m, c)
+        for k in range(2, batches):
+
+            @pl.when(jnp.logical_and(section == 0, t == k - 1))
+            def _(k=k):
+                release(k, 1 if k == 2 else 2)
+
+        for op, i in PLAN:
+            if op == "combine":
+
+                @pl.when(t > 0)
+                def _(i=i):
+                    for c in range(i * group, (i + 1) * group):
+                        combine(m, c)
+
+            elif op == "turn":
+
+                @pl.when(t > 0)
+                def _():
+                    hand_over(m)
+
+            elif op == "relay":
+                due = jnp.logical_and(t > 0, jnp.logical_and(active, section > 0))
+
+                @pl.when(jnp.logical_and(due, halved(jnp.minimum(t, batches - 1))))
+                def _(i=i):
+                    pass_on(t, range(i * group, (i + 1) * group))
+
+            else:
+
+                @pl.when(active)
+                def _(i=i):
+                    stages[i](t)
 
         return carry
 
@@ -411,7 +526,7 @@
         def drain(c, carry):
             for g in range(1, group):
 
-                @pl.when(part_needed(m, c, g))
+                @pl.when(jnp.logical_and(c >= SENT, part_needed(m, c, g)))
                 def _():
                     part_copy(m, c, g).wait_send()
 
@@ -419,10 +534,17 @@
             def _():
                 next_copy(m, c).wait_send()
 
-            @pl.when(jnp.logical_and(m == 0, lax.rem(c, group) == member))
+            @pl.when(jnp.logical_and(halved(m), lax.rem(c, group) == member))
             def _():
                 for g in range(1, group):
-                    relay(c, g).wait_send()
+                    relay(m, c, g).wait_send()
+
+            @pl.when(jnp.logical_and(is_cross, lax.rem(c, group) == member))
+            def _():
+                @pl.when(c // group != 2)
+                def _():
+                    for g in range(1, group):
+                        cross_relay(m, c, g).wait_send()
 
             @pl.when(jnp.logical_and(is_last, jnp.logical_and(keeps(m, c), me != c)))
             def _():
@@ -475,12 +597,14 @@
                 dma((batches, group - 1, segs)),
                 dma((batches, segs)),
                 dma((batches,)),
-                pltpu.SemaphoreType.REGULAR,
+                pltpu.SemaphoreType.REGULAR((batches - 1,)),
                 pltpu.VMEM((batches - 1, group - 1, seq, cw), bf16),
                 dma((batches - 1, group - 1)),
                 dma((batches - 1, group - 1)),
                 dma((batches - 1, group - 1)),
-                dma((group - 1, segs)),
+                dma((batches, group - 1, segs)),
+                dma((batches, group - 1, segs)),
+                pltpu.SemaphoreType.REGULAR,
             ],
             compiler_params=pltpu.CompilerParams(
                 collective_id=0,

time: 131 us -> 115 us (0.88)
  Pallas kernels: 129 us -> 113 us
    pallas_call x1, Pallas kernels: 129 us -> 113 us  [on_device(): pl.pallas_call(functools.partial(kernel, segs), out_shape=jax.ShapeDtypeS...]
where the time goes in v1:
time: 115 us; the launch traced here: 114 us
  Pallas kernels  113 us (98%)
  local copies, waits for them, and re-layouts  1.67 us (1%)
    pallas_call x1, Pallas kernels, on_device(): pl.pallas_call(functools.partial(kernel, segs), out_shape=jax.ShapeDtypeS...  113 us

profile of v1, /device:TPU:0, one launch (start us, length us, event | category | flops | bytes accessed | tf_op | source)
XLA Modules:
  0.0 114.4 jit_solution(15200555400706563448)
XLA Ops:
  0.0 112.7 %shard_map.82 = bf16[4,128,256]{2,1,0:T(8,128)(2,1)} custom-call(s32[4]{0:T(128)} %src_len.1, s32[4]{0:T(128)} %tgt_len.1, bf16[4,128,256]{2,1,0:T(8,128)(2,1)} %src.1, bf16[4,128,256]{2,1,0:T(8,128)(2,1)} %tgt.1, bf16[2048,3072]{1,0:T(8,128)(2,1)} %bitcast.3, bf16[1024,2048]{1,0:T(8,128)(2,1)} %bitcast.4, f32[4,2048]{1,0:T(4,128)} %gains.1, f32[1,2048]{1,0:T(1,128)} %bitcast.5), custom_call_target="tpu_custom_call" | custom-call | tf_op jit(solution)/shard_map/pallas_call | solution.py:577
  112.7 1.7 %copy.10 = bf16[4,128,256]{2,1,0:T(8,128)(2,1)} copy(bf16[4,128,256]{2,1,0:T(8,128)(2,1)} %shard_map.82) | data formatting | bytes 524288

commit v2 on v1

--- a/solution.py
+++ b/solution.py
@@ -10,18 +10,7 @@
 HEAD = 64
 LAYERS = 4
 MESH = pl.DeviceIdType.MESH
-SENT = 2
-PLAN = (
-    ("turn", 0),
-    ("combine", 0),
-    ("combine", 1),
-    ("combine", 2),
-    ("combine", 3),
-    ("stage", 0),
-    ("stage", 1),
-    ("stage", 2),
-    ("stage", 3),
-)
+TURN = 0
 epsilon = 1e-06
 score_scale = 0.125
 
@@ -47,20 +36,24 @@
     ps,
     pr,
     fw,
+    side,
     w_sem,
-    act_sem,
+    first_own,
+    first_rest,
+    later,
+    tgt_own,
+    tgt_rest,
     in_send,
     p_send,
     p_recv,
     f_send,
     o_recv,
-    go,
-    side,
     side_send,
     side_recv,
     on_send,
     r_send,
     t_send,
+    go,
     turn,
 ):
     group = segs // LAYERS
@@ -105,15 +98,27 @@
             device_id_type=MESH,
         )
 
+    def enc_sem(m, owned, c):
+        if isinstance(m, int) and m > 0:
+            return later.at[m]
+        return first_own.at[c // group] if owned else first_rest.at[0]
+
     def input_copy(kind, m, j):
         ref = src if kind == 0 else tgt
         target = 2 * kind * group + j
+        if kind == 0:
+            recv = enc_sem(m, True, me)
+        else:
+            recv = tgt_own.at[m, section]
+        return remote(ref.at[m], act.at[kind, m, me], in_send.at[kind], recv, target)
+
+    def share_copy(m, j):
         return remote(
-            ref.at[m],
-            act.at[kind, m, me],
-            in_send.at[kind, m, j],
-            act_sem.at[kind, m, me],
-            target,
+            tgt.at[m],
+            act.at[1, m, me],
+            in_send.at[1],
+            tgt_rest.at[m],
+            2 * group + j,
         )
 
     def sends(kind, m, j):
@@ -125,15 +130,24 @@
         ref = src if kind == 0 else tgt
         for j in range(group):
             target = 2 * kind * group + j
-
-            @pl.when(jnp.logical_and(sends(kind, m, j), me != target))
+            wanted = jnp.logical_and(sends(kind, m, j), me != target)
+            if kind == 1:
+
+                @pl.when(jnp.logical_and(wanted, is_cross))
+                def _():
+                    share_copy(m, j).start()
+
+                wanted = jnp.logical_and(wanted, jnp.logical_not(is_cross))
+
+            @pl.when(wanted)
             def _():
                 input_copy(kind, m, j).start()
 
             @pl.when(me == target)
             def _():
+                own_sem = enc_sem(m, True, j) if kind == 0 else tgt_own.at[m, 2]
                 pltpu.make_async_copy(
-                    ref.at[m], act.at[kind, m, me], act_sem.at[kind, m, me]
+                    ref.at[m], act.at[kind, m, me], own_sem
                 ).start()
 
     def beside(g):
@@ -143,7 +157,7 @@
         return remote(
             src.at[m],
             side.at[m - 1, g - 1],
-            side_send.at[m - 1, g - 1],
+            side_send.at[g - 1],
             side_recv.at[m - 1, g - 1],
             beside(g),
         )
@@ -153,19 +167,22 @@
         return remote(
             side.at[m - 1, g - 1],
             act.at[0, m, source],
-            on_send.at[m - 1, g - 1],
-            act_sem.at[0, m, source],
+            on_send.at[g - 1],
+            later.at[m],
             member,
         )
 
-    def relay(m, c, g):
+    def relay(c, g):
         return remote(
-            act.at[0, m, c],
-            act.at[0, m, c],
-            r_send.at[m, g - 1, c],
-            act_sem.at[0, m, c],
+            act.at[0, 0, c],
+            act.at[0, 0, c],
+            r_send.at[g - 1],
+            first_rest.at[0],
             beside(g),
         )
+
+    def wait_bytes(ref, sem):
+        pltpu.make_async_copy(ref, ref, sem).wait()
 
     send_inputs(0, 0)
 
@@ -180,19 +197,14 @@
         for m in range(batches):
             send_inputs(1, m)
 
-    def act_wait(kind, m, c):
-        pltpu.make_async_copy(
-            act.at[kind, m, c], act.at[kind, m, c], act_sem.at[kind, m, c]
-        ).wait()
-
-    def pass_on(m, order):
+    def pass_on(order):
         for c in order:
 
             @pl.when(c % group == member)
             def _(c=c):
-                act_wait(0, m, c)
+                wait_bytes(act.at[0, 0, c], first_own.at[c // group])
                 for g in range(1, group):
-                    relay(m, c, g).start()
+                    relay(c, g).start()
 
     def release(k, first):
         for c in range(first * group, segs):
@@ -208,16 +220,16 @@
 
     @pl.when(section == 0)
     def _():
-        pass_on(0, tuple(range(group)) + tuple(range(segs - 1, 2 * group - 1, -1)))
+        pass_on(tuple(range(group)) + tuple(range(segs - 1, 2 * group - 1, -1)))
         release(1, 0)
-        pass_on(0, range(group, 2 * group))
+        pass_on(range(group, 2 * group))
 
     def cross_relay(m, c, g):
         return remote(
             act.at[1, m, c],
             act.at[1, m, c],
-            t_send.at[m, g - 1, c],
-            act_sem.at[1, m, c],
+            t_send.at[g - 1],
+            tgt_rest.at[m],
             beside(g),
         )
 
@@ -228,7 +240,7 @@
 
                     @pl.when(jnp.logical_and(is_cross, c % group == member))
                     def _(m=m, c=c, p=p):
-                        act_wait(1, m, c)
+                        wait_bytes(act.at[1, m, c], tgt_own.at[m, p])
                         if p != 2:
                             for g in range(1, group):
                                 cross_relay(m, c, g).start()
@@ -289,7 +301,7 @@
         return remote(
             ps.at[m, c],
             pr.at[m, g - 1, c],
-            p_send.at[m, g - 1, c],
+            p_send.at[m, g - 1, jnp.where(c < group, 0, 1)],
             p_recv.at[m, g - 1, c],
             target,
         )
@@ -301,10 +313,6 @@
     def whole(m):
         return whole_from(section, m)
 
-    def halved(m):
-        later = jnp.logical_and(section > 0, jnp.logical_not(whole_from(section - 1, m)))
-        return jnp.logical_or(m == 0, later)
-
     def part_needed(m, c, g):
         goal = lax.rem(member + g, group)
         return jnp.logical_or(whole(m), lax.rem(c, group) == goal)
@@ -312,13 +320,11 @@
     def keeps(m, c):
         return jnp.logical_or(whole(m), lax.rem(c, group) == member)
 
-    def next_copy(m, c):
-        return remote(
-            fw.at[m, c], act.at[0, m, c], f_send.at[m, c], act_sem.at[0, m, c], me + group
-        )
+    def next_copy(m, c, recv):
+        return remote(fw.at[m, c], act.at[0, m, c], f_send.at[m], recv, me + group)
 
     def out_copy(m, c):
-        return remote(fw.at[m, c], out.at[m], f_send.at[m, c], o_recv.at[m], c)
+        return remote(fw.at[m, c], out.at[m], f_send.at[m], o_recv.at[0], c)
 
     tile = min(512, hc)
     kv_tiles = 2 * hc // tile
@@ -327,30 +333,25 @@
     def prepare(m):
         @pl.when(is_cross)
         def _():
-            for c in range(segs):
-
-                @pl.when(c % group != member)
-                def _(c=c):
-                    act_wait(1, m, c)
-
+            wait_bytes(act.at[1, m, pl.ds(0, segs - LAYERS)], tgt_rest.at[m])
             normalize(1, m, query_gain)
 
         @pl.when(jnp.logical_and(section > 0, m == 0))
         def _():
-            pass_on(0, range(segs))
-
-        for c in range(segs):
-
-            @pl.when(jnp.logical_not(jnp.logical_and(halved(m), c % group == member)))
-            def _(c=c):
-                act_wait(0, m, c)
+            pass_on(range(segs))
+
+        @pl.when(m == 0)
+        def _():
+            wait_bytes(act.at[0, 0, pl.ds(0, segs - LAYERS)], first_rest.at[0])
+
+        @pl.when(m > 0)
+        def _():
+            wait_bytes(act.at[0, m], later.at[m])
 
         normalize(0, m, key_gain)
-
         @pl.when(m == 0)
         def _():
             win_copy.wait()
-
 
     def project(t, carry):
         kind = jnp.where(t < q_tiles, q_src, 0)
@@ -360,7 +361,7 @@
         ).astype(jnp.bfloat16)
         return carry
 
-    def attend(m):
+    def attend(m, pairs):
         length = jnp.where(is_last, tgt_len[m], src_len[m])
         keys = lax.broadcasted_iota(jnp.int32, (2 * seq, seq), 1)
         rows = lax.broadcasted_iota(jnp.int32, (2 * seq, seq), 0)
@@ -369,7 +370,7 @@
         allowed = (keys < length) & (keys <= bound)
         lane = lax.broadcasted_iota(jnp.int32, (seq, 2 * HEAD), 1)
         low = lane < HEAD
-        for h in range(hc // (2 * HEAD)):
+        for h in pairs:
             at = h * 2 * HEAD
             q2 = qkv[:, at : at + 2 * HEAD]
             k2 = qkv[:, hc + at : hc + at + 2 * HEAD]
@@ -421,13 +422,20 @@
 
         lax.fori_loop(0, segs, emit, 0, unroll=True)
 
+    def part_sends(m, at, count, count_half):
+        for g in range(1, group):
+            sem = p_send.at[m, g - 1, at]
+
+            @pl.when(whole(m))
+            def _():
+                wait_bytes(ps.at[m, pl.ds(0, count)], sem)
+
+            @pl.when(jnp.logical_not(whole(m)))
+            def _():
+                wait_bytes(ps.at[m, pl.ds(0, count_half)], sem)
+
     def hand_over(m):
-        for c in range(SENT):
-            for g in range(1, group):
-
-                @pl.when(part_needed(m, c, g))
-                def _(c=c, g=g):
-                    part_copy(m, c, g).wait_send()
+        part_sends(m, 0, group, 1)
 
         @pl.when(jnp.logical_or(m < batches - 1, leads))
         def _():
@@ -444,9 +452,15 @@
                 total = total + pr[m, g - 1, c].astype(jnp.float32)
             fw[m, c] = total.astype(jnp.bfloat16)
 
-            @pl.when(section < LAYERS - 1)
-            def _():
-                next_copy(m, c).start()
+            onward = section < LAYERS - 1
+
+            @pl.when(jnp.logical_and(onward, m == 0))
+            def _():
+                next_copy(m, c, first_own.at[c // group]).start()
+
+            @pl.when(jnp.logical_and(onward, m > 0))
+            def _():
+                next_copy(m, c, later.at[m]).start()
 
             @pl.when(jnp.logical_and(is_last, me != c))
             def _():
@@ -454,19 +468,40 @@
 
             @pl.when(jnp.logical_and(is_last, me == c))
             def _():
-                pltpu.make_async_copy(fw.at[m, c], out.at[m], o_recv.at[m]).start()
-
-    half = (q_tiles + kv_tiles) // 2
-    stages = (
-        prepare,
-        lambda m: lax.fori_loop(0, half, project, 0, unroll=True),
-        lambda m: lax.fori_loop(half, q_tiles + kv_tiles, project, 0, unroll=True),
-        attend,
-    )
+                pltpu.make_async_copy(fw.at[m, c], out.at[m], o_recv.at[0]).start()
+
+    tiles = q_tiles + kv_tiles
+    head_pairs = hc // (2 * HEAD)
+
+    def run(step, m, t):
+        kind, i, n = step
+        if kind == "turn":
+            pl.when(t > 0)(lambda: hand_over(m))
+        elif kind == "combine":
+            pl.when(t > 0)(lambda: combine(m, i))
+        elif kind == "prepare":
+            pl.when(t < batches)(lambda: prepare(t))
+        elif kind == "project":
+
+            @pl.when(t < batches)
+            def _():
+                lo, hi = i * tiles // n, (i + 1) * tiles // n
+                lax.fori_loop(lo, hi, project, 0, unroll=True)
+
+        else:
+
+            @pl.when(t < batches)
+            def _():
+                attend(t, range(i * head_pairs // n, (i + 1) * head_pairs // n))
+
+    combines = [("combine", c, segs) for c in range(segs)]
+    turn_at = min(TURN, segs - 1)
+    steps = combines[:turn_at] + [("turn", 0, 1)] + combines[turn_at:]
+    steps += [("prepare", 0, 1)]
+    steps += [("project", 0, 2), ("project", 1, 2), ("attend", 0, 1)]
 
     def batch_step(t, carry):
         m = t - 1
-        active = t < batches
 
         @pl.when(t > 0)
         def _():
@@ -478,85 +513,54 @@
             def _(k=k):
                 release(k, 1 if k == 2 else 2)
 
-        for op, i in PLAN:
-            if op == "combine":
-
-                @pl.when(t > 0)
-                def _(i=i):
-                    for c in range(i * group, (i + 1) * group):
-                        combine(m, c)
-
-            elif op == "turn":
-
-                @pl.when(t > 0)
-                def _():
-                    hand_over(m)
-
-            elif op == "relay":
-                due = jnp.logical_and(t > 0, jnp.logical_and(active, section > 0))
-
-                @pl.when(jnp.logical_and(due, halved(jnp.minimum(t, batches - 1))))
-                def _(i=i):
-                    pass_on(t, range(i * group, (i + 1) * group))
-
-            else:
-
-                @pl.when(active)
-                def _(i=i):
-                    stages[i](t)
+        for step in steps:
+            run(step, m, t)
 
         return carry
 
     lax.fori_loop(0, batches + 1, batch_step, 0)
 
-    def finish(m, carry):
-        for kind in range(2):
-            for j in range(group):
-
-                @pl.when(jnp.logical_and(sends(kind, m, j), me != 2 * kind * group + j))
-                def _():
-                    input_copy(kind, m, j).wait_send()
-
-        @pl.when(jnp.logical_and(section > 0, m > 0))
-        def _():
-            for g in range(1, group):
-                side_copy(m, g).wait_send()
-                side_on(m, g).wait_send()
-
-        def drain(c, carry):
-            for g in range(1, group):
-
-                @pl.when(jnp.logical_and(c >= SENT, part_needed(m, c, g)))
-                def _():
-                    part_copy(m, c, g).wait_send()
-
-            @pl.when(jnp.logical_and(section < LAYERS - 1, keeps(m, c)))
-            def _():
-                next_copy(m, c).wait_send()
-
-            @pl.when(jnp.logical_and(halved(m), lax.rem(c, group) == member))
-            def _():
-                for g in range(1, group):
-                    relay(m, c, g).wait_send()
-
-            @pl.when(jnp.logical_and(is_cross, lax.rem(c, group) == member))
-            def _():
-                @pl.when(c // group != 2)
-                def _():
-                    for g in range(1, group):
-                        cross_relay(m, c, g).wait_send()
-
-            @pl.when(jnp.logical_and(is_last, jnp.logical_and(keeps(m, c), me != c)))
-            def _():
-                out_copy(m, c).wait_send()
-
-            return carry
-
-        lax.fori_loop(0, segs, drain, 0)
-        pltpu.make_async_copy(out.at[m], out.at[m], o_recv.at[m]).wait()
-        return carry
-
-    lax.fori_loop(0, batches, finish, 0)
+    def forward_sends(m):
+        for ahead, count in ((whole(m), segs), (jnp.logical_not(whole(m)), LAYERS)):
+
+            @pl.when(jnp.logical_and(section < LAYERS - 1, ahead))
+            def _(count=count):
+                wait_bytes(fw.at[m, pl.ds(0, count)], f_send.at[m])
+
+        @pl.when(is_last)
+        def _():
+            wait_bytes(fw.at[m, pl.ds(0, LAYERS - 1)], f_send.at[m])
+
+    some = pl.ds(0, batches - 1)
+    for m in range(batches):
+        part_sends(m, 1, segs - group, LAYERS - 1)
+        forward_sends(m)
+
+    @pl.when(section > 0)
+    def _():
+        wait_bytes(src, in_send.at[0])
+        for g in range(1, group):
+            wait_bytes(src.at[some], side_send.at[g - 1])
+            wait_bytes(src.at[some], on_send.at[g - 1])
+
+    @pl.when(section == 0)
+    def _():
+        for g in range(1, group):
+            wait_bytes(src.at[some], in_send.at[0])
+
+    @pl.when(jnp.logical_not(is_cross))
+    def _():
+        wait_bytes(tgt, in_send.at[1])
+
+    for g in range(1, group):
+        wait_bytes(act.at[0, 0, pl.ds(0, LAYERS)], r_send.at[g - 1])
+
+        @pl.when(is_cross)
+        def _(g=g):
+            wait_bytes(tgt, in_send.at[1])
+            wait_bytes(act.at[1, :, pl.ds(0, LAYERS - 1)], t_send.at[g - 1])
+
+    wait_bytes(out, o_recv.at[0])
 
 
 def solution(mesh):
@@ -576,7 +580,7 @@
         dma = pltpu.SemaphoreType.DMA
         return pl.pallas_call(
             functools.partial(kernel, segs),
-            out_shape=jax.ShapeDtypeStruct(src.shape, src.dtype),
+            out_shape=pltpu.VMEM(src.shape, src.dtype),
             in_specs=[smem, smem, vmem, vmem, anym, anym, vmem, vmem],
             out_specs=vmem,
             scratch_shapes=[
@@ -590,20 +594,24 @@
                 pltpu.VMEM((batches,) + block, bf16),
                 pltpu.VMEM((batches, group - 1) + block, bf16),
                 pltpu.VMEM((batches,) + block, bf16),
+                pltpu.VMEM((batches - 1, group - 1, seq, cw), bf16),
                 dma((2,)),
-                dma((2, batches, segs)),
-                dma((2, batches, group)),
+                dma((LAYERS,)),
+                dma((1,)),
+                dma((batches,)),
+                dma((batches, LAYERS)),
+                dma((batches,)),
+                dma((2,)),
+                dma((batches, group - 1, 2)),
                 dma((batches, group - 1, segs)),
-                dma((batches, group - 1, segs)),
-                dma((batches, segs)),
                 dma((batches,)),
+                dma((1,)),
+                dma((group - 1,)),
+                dma((batches - 1, group - 1)),
+                dma((group - 1,)),
+                dma((group - 1,)),
+                dma((group - 1,)),
                 pltpu.SemaphoreType.REGULAR((batches - 1,)),
-                pltpu.VMEM((batches - 1, group - 1, seq, cw), bf16),
-                dma((batches - 1, group - 1)),
-                dma((batches - 1, group - 1)),
-                dma((batches - 1, group - 1)),
-                dma((batches, group - 1, segs)),
-                dma((batches, group - 1, segs)),
                 pltpu.SemaphoreType.REGULAR,
             ],
             compiler_params=pltpu.CompilerParams(

time: 115 us -> 111 us (0.965)
  Pallas kernels: 113 us -> 110 us
    pallas_call x1, Pallas kernels: 113 us -> 110 us  [on_device(): pl.pallas_call(functools.partial(kernel, segs), out_shape=pltpu.VMEM(src....]
where the time goes in v2:
time: 111 us
  Pallas kernels  110 us (99%)
    pallas_call x1, Pallas kernels, on_device(): pl.pallas_call(functools.partial(kernel, segs), out_shape=pltpu.VMEM(src....  110 us

profile of v2, /device:TPU:0, one launch (start us, length us, event | category | flops | bytes accessed | tf_op | source)
XLA Modules:
  0.0 110.9 jit_solution(2255100940848476868)
XLA Ops:
  0.0 110.1 %shard_map.82 = bf16[4,128,256]{2,1,0:T(8,128)(2,1)S(1)} custom-call(s32[4]{0:T(128)} %src_len.1, s32[4]{0:T(128)} %tgt_len.1, bf16[4,128,256]{2,1,0:T(8,128)(2,1)} %src.1, bf16[4,128,256]{2,1,0:T(8,128)(2,1)} %tgt.1, bf16[2048,3072]{1,0:T(8,128)(2,1)} %bitcast.3, bf16[1024,2048]{1,0:T(8,128)(2,1)} %bitcast.4, f32[4,2048]{1,0:T(4,128)} %gains.1, ...), custom_call_target="tpu_custom_call" | custom-call | tf_op jit(solution)/shard_map/pallas_call | solution.py:581
  110.1 0.7 copy.10

commit v3 on v2

--- a/solution.py
+++ b/solution.py
@@ -37,6 +37,7 @@
     pr,
     fw,
     side,
+    acc,
     w_sem,
     first_own,
     first_rest,
@@ -98,16 +99,16 @@
             device_id_type=MESH,
         )
 
-    def enc_sem(m, owned, c):
+    def enc_sem(m, c):
         if isinstance(m, int) and m > 0:
             return later.at[m]
-        return first_own.at[c // group] if owned else first_rest.at[0]
+        return first_own.at[c // group]
 
     def input_copy(kind, m, j):
         ref = src if kind == 0 else tgt
         target = 2 * kind * group + j
         if kind == 0:
-            recv = enc_sem(m, True, me)
+            recv = enc_sem(m, me)
         else:
             recv = tgt_own.at[m, section]
         return remote(ref.at[m], act.at[kind, m, me], in_send.at[kind], recv, target)
@@ -145,7 +146,7 @@
 
             @pl.when(me == target)
             def _():
-                own_sem = enc_sem(m, True, j) if kind == 0 else tgt_own.at[m, 2]
+                own_sem = enc_sem(m, j) if kind == 0 else tgt_own.at[m, 2]
                 pltpu.make_async_copy(
                     ref.at[m], act.at[kind, m, me], own_sem
                 ).start()
@@ -177,7 +178,7 @@
             act.at[0, 0, c],
             act.at[0, 0, c],
             r_send.at[g - 1],
-            first_rest.at[0],
+            first_rest.at[c],
             beside(g),
         )
 
@@ -220,7 +221,9 @@
 
     @pl.when(section == 0)
     def _():
-        pass_on(tuple(range(group)) + tuple(range(segs - 1, 2 * group - 1, -1)))
+        pass_on(range(group))
+        send_inputs(0, 1)
+        pass_on(range(segs - 1, 2 * group - 1, -1))
         release(1, 0)
         pass_on(range(group, 2 * group))
 
@@ -254,7 +257,9 @@
             def _(m=m):
                 pl.semaphore_wait(go.at[m - 1], group)
 
-        send_inputs(0, m)
+        @pl.when(section > 0)
+        def _(m=m):
+            send_inputs(0, m)
 
         @pl.when(section > 0)
         def _(m=m):
@@ -287,7 +292,7 @@
             nrm[kind, :, c * cw : (c + 1) * cw] = (v * scale * g).astype(jnp.bfloat16)
 
     def key_gain(c):
-        cols = slice(c * cw, (c + 1) * cw)
+        cols = pl.ds(pl.multiple_of(c * cw, cw), cw)
         picked = jnp.where(is_cross, final_gain[:, cols], gains[0:1, cols])
         for p in (1, 3):
             picked = jnp.where(section == p, gains[p : p + 1, cols], picked)
@@ -326,40 +331,23 @@
     def out_copy(m, c):
         return remote(fw.at[m, c], out.at[m], f_send.at[m], o_recv.at[0], c)
 
-    tile = min(512, hc)
-    kv_tiles = 2 * hc // tile
-    q_tiles = hc // tile
-
     def prepare(m):
         @pl.when(is_cross)
         def _():
             wait_bytes(act.at[1, m, pl.ds(0, segs - LAYERS)], tgt_rest.at[m])
             normalize(1, m, query_gain)
 
-        @pl.when(jnp.logical_and(section > 0, m == 0))
-        def _():
-            pass_on(range(segs))
-
-        @pl.when(m == 0)
-        def _():
-            wait_bytes(act.at[0, 0, pl.ds(0, segs - LAYERS)], first_rest.at[0])
-
         @pl.when(m > 0)
         def _():
             wait_bytes(act.at[0, m], later.at[m])
-
-        normalize(0, m, key_gain)
-        @pl.when(m == 0)
-        def _():
-            win_copy.wait()
-
-    def project(t, carry):
-        kind = jnp.where(t < q_tiles, q_src, 0)
-        cols = pl.ds(pl.multiple_of(t * tile, tile), tile)
+            normalize(0, m, key_gain)
+
+    def project(at, width_at):
+        kind = q_src if at < hc else 0
+        cols = slice(at, at + width_at)
         qkv[:, cols] = jnp.dot(
             nrm[kind], win[:, cols], preferred_element_type=jnp.float32
         ).astype(jnp.bfloat16)
-        return carry
 
     def attend(m, pairs):
         length = jnp.where(is_last, tgt_len[m], src_len[m])
@@ -391,7 +379,7 @@
             scores = jnp.where(allowed, scores, -1000000000.0)
             top = jnp.max(scores, axis=-1, keepdims=True)
             e = jnp.exp(scores - top)
-            weights = (e / jnp.sum(e, axis=-1, keepdims=True)).astype(jnp.bfloat16)
+            weights = (e * (1.0 / jnp.sum(e, axis=-1, keepdims=True))).astype(jnp.bfloat16)
             o = jnp.dot(weights, v2, preferred_element_type=jnp.float32)
             mix[:, at : at + 2 * HEAD] = jnp.where(low, o[:seq], o[seq:]).astype(
                 jnp.bfloat16
@@ -470,8 +458,70 @@
             def _():
                 pltpu.make_async_copy(fw.at[m, c], out.at[m], o_recv.at[0]).start()
 
-    tiles = q_tiles + kv_tiles
     head_pairs = hc // (2 * HEAD)
+    tile = min(512, hc)
+
+    def add_chunk(c, first):
+        v = act[0, 0, c].astype(jnp.float32)
+        square = v * v
+        own[0] = square if first else own[0] + square
+        scaled = (v * key_gain(c)).astype(jnp.bfloat16)
+        rows = pl.ds(pl.multiple_of(c * cw, cw), cw)
+        for at in range(0, 3 * hc, tile):
+            cols = slice(at, at + tile)
+            part = jnp.dot(
+                scaled, win[rows, cols], preferred_element_type=jnp.float32
+            )
+            acc[:, cols] = part if first else acc[:, cols] + part
+
+    def start_up():
+        @pl.when(section == 0)
+        def _():
+            for k in range(2, batches):
+                send_inputs(0, k)
+
+        win_copy.wait()
+
+        @pl.when(is_cross)
+        def _():
+            for at in range(0, hc, tile):
+                project(at, tile)
+
+        for i in range(LAYERS):
+            c = i * group + member
+
+            @pl.when(section > 0)
+            def _(i=i, c=c):
+                wait_bytes(act.at[0, 0, c], first_own.at[i])
+                for g in range(1, group):
+                    relay(c, g).start()
+
+            add_chunk(c, i == 0)
+        for i in range(LAYERS):
+            for g in range(1, group):
+                c = i * group + lax.rem(member + g, group)
+                wait_bytes(act.at[0, 0, c], first_rest.at[c])
+                add_chunk(c, False)
+        mean = jnp.sum(own[0], axis=-1, keepdims=True) * (1.0 / width)
+        scale = lax.rsqrt(mean + epsilon)
+
+        @pl.when(jnp.logical_not(is_cross))
+        def _():
+            qkv[:, :hc] = (acc[:, :hc] * scale).astype(jnp.bfloat16)
+
+        qkv[:, hc:] = (acc[:, hc:] * scale).astype(jnp.bfloat16)
+
+    def compute(m):
+        @pl.when(m == 0)
+        def _():
+            start_up()
+            attend(m, range(head_pairs))
+
+        @pl.when(m > 0)
+        def _():
+            for at in range(0, 3 * hc, tile):
+                project(at, tile)
+            attend(m, range(head_pairs))
 
     def run(step, m, t):
         kind, i, n = step
@@ -481,24 +531,13 @@
             pl.when(t > 0)(lambda: combine(m, i))
         elif kind == "prepare":
             pl.when(t < batches)(lambda: prepare(t))
-        elif kind == "project":
-
-            @pl.when(t < batches)
-            def _():
-                lo, hi = i * tiles // n, (i + 1) * tiles // n
-                lax.fori_loop(lo, hi, project, 0, unroll=True)
-
         else:
-
-            @pl.when(t < batches)
-            def _():
-                attend(t, range(i * head_pairs // n, (i + 1) * head_pairs // n))
+            pl.when(t < batches)(lambda: compute(t))
 
     combines = [("combine", c, segs) for c in range(segs)]
     turn_at = min(TURN, segs - 1)
     steps = combines[:turn_at] + [("turn", 0, 1)] + combines[turn_at:]
-    steps += [("prepare", 0, 1)]
-    steps += [("project", 0, 2), ("project", 1, 2), ("attend", 0, 1)]
+    steps += [("prepare", 0, 1), ("compute", 0, 1)]
 
     def batch_step(t, carry):
         m = t - 1
@@ -595,9 +634,10 @@
                 pltpu.VMEM((batches, group - 1) + block, bf16),
                 pltpu.VMEM((batches,) + block, bf16),
                 pltpu.VMEM((batches - 1, group - 1, seq, cw), bf16),
+                pltpu.VMEM((seq, qkv_cols), jnp.float32),
                 dma((2,)),
                 dma((LAYERS,)),
-                dma((1,)),
+                dma((segs,)),
                 dma((batches,)),
                 dma((batches, LAYERS)),
                 dma((batches,)),

time: 111 us -> 110 us (level)
  no operation moved by 1% of the time
where the time goes in v3:
time: 110 us
  Pallas kernels  110 us (100%)
    pallas_call x1, Pallas kernels, on_device(): pl.pallas_call(functools.partial(kernel, segs), out_shape=pltpu.VMEM(src....  110 us

profile of v3, /device:TPU:0, one launch (start us, length us, event | category | flops | bytes accessed | tf_op | source)
XLA Modules:
  0.0 110.3 jit_solution(17412766080793379003)
XLA Ops:
  0.0 109.5 %shard_map.82 = bf16[4,128,256]{2,1,0:T(8,128)(2,1)S(1)} custom-call(s32[4]{0:T(128)} %src_len.1, s32[4]{0:T(128)} %tgt_len.1, bf16[4,128,256]{2,1,0:T(8,128)(2,1)} %src.1, bf16[4,128,256]{2,1,0:T(8,128)(2,1)} %tgt.1, bf16[2048,3072]{1,0:T(8,128)(2,1)} %bitcast.3, bf16[1024,2048]{1,0:T(8,128)(2,1)} %bitcast.4, f32[4,2048]{1,0:T(4,128)} %gains.1, ...), custom_call_target="tpu_custom_call" | custom-call | tf_op jit(solution)/shard_map/pallas_call | solution.py:620
  109.6 0.7 copy.10

commit v4 on v3

--- a/solution.py
+++ b/solution.py
@@ -423,8 +423,6 @@
                 wait_bytes(ps.at[m, pl.ds(0, count_half)], sem)
 
     def hand_over(m):
-        part_sends(m, 0, group, 1)
-
         @pl.when(jnp.logical_or(m < batches - 1, leads))
         def _():
             pl.semaphore_signal(
@@ -572,6 +570,7 @@
 
     some = pl.ds(0, batches - 1)
     for m in range(batches):
+        part_sends(m, 0, group, 1)
         part_sends(m, 1, segs - group, LAYERS - 1)
         forward_sends(m)
 

time: 110 us -> 110 us (level)
  no operation moved by 1% of the time
where the time goes in v4:
time: 110 us
  Pallas kernels  109 us (99%)
    pallas_call x1, Pallas kernels, on_device(): pl.pallas_call(functools.partial(kernel, segs), out_shape=pltpu.VMEM(src....  109 us

profile of v4, /device:TPU:0, one launch (start us, length us, event | category | flops | bytes accessed | tf_op | source)
XLA Modules:
  0.0 110.1 jit_solution(14912246050037931940)
XLA Ops:
  0.0 109.4 %shard_map.82 = bf16[4,128,256]{2,1,0:T(8,128)(2,1)S(1)} custom-call(s32[4]{0:T(128)} %src_len.1, s32[4]{0:T(128)} %tgt_len.1, bf16[4,128,256]{2,1,0:T(8,128)(2,1)} %src.1, bf16[4,128,256]{2,1,0:T(8,128)(2,1)} %tgt.1, bf16[2048,3072]{1,0:T(8,128)(2,1)} %bitcast.3, bf16[1024,2048]{1,0:T(8,128)(2,1)} %bitcast.4, f32[4,2048]{1,0:T(4,128)} %gains.1, ...), custom_call_target="tpu_custom_call" | custom-call | tf_op jit(solution)/shard_map/pallas_call | solution.py:619
  109.4 0.7 copy.10
